TPU v7x, 32 devices: a whole 2x2x4 slice. The times are simulated.
32 devices in a mesh: g: 32 (over z, y, x, core).
Axes of the slice: x: 2, y: 2, z: 4, core: 2. Of those that a mesh axis runs over, the one named last changes fastest.
Arguments:
- node_feat: bfloat16 [16384, 8448], P(None, 'g')
- w_self1: bfloat16 [8448, 256], P('g')
- w_nbr1: bfloat16 [8448, 256], P('g')
- nbr_ids: int32 [16384, 15], P('g')
- nbr_mask: int32 [16384, 15], P('g')
- w_self2: bfloat16 [256, 256], replicated
- w_nbr2: bfloat16 [256, 256], replicated
- w_self3: bfloat16 [256, 5], replicated
- w_nbr3: bfloat16 [256, 5], replicated
Outputs:
- output: float32 [16384, 5], P('g')
All inputs are finite; a program needn't handle non-finite values.
Results may differ from a plain program's by a relative error of at most 0.00945678.
Values are sent between devices in bfloat16 or wider.
A program may use at most 1 GiB of HBM per device.

v0:
```python
import jax
import jax.numpy as jnp
from jax import lax
from jax.sharding import PartitionSpec as P, NamedSharding


def slot_total(row_data, nbr_ids, mask_f):
    def add_slot(acc_sum, slot_cols):
        ids_col, mask_col = slot_cols
        picked = jnp.take(row_data, ids_col, axis=0).astype(jnp.float32)
        return acc_sum + mask_col[:, None] * picked, None

    zero_acc = jnp.zeros((nbr_ids.shape[0], row_data.shape[1]), jnp.float32)
    slot_sum, _ = lax.scan(add_slot, zero_acc, (nbr_ids.T, mask_f.T))
    return slot_sum


def solution(mesh):
    def device_step(feat_cols, self_rows1, nbr_rows1, ids_local, mask_local, w_self2, w_nbr2, w_self3, w_nbr3):
        ids_all = lax.all_gather(ids_local, "g", tiled=True)
        mask_all = lax.all_gather(mask_local, "g", tiled=True).astype(jnp.float32)
        inv_all = 1.0 / jnp.sum(mask_all, axis=1, keepdims=True)
        self_part = jnp.dot(feat_cols, self_rows1, preferred_element_type=jnp.float32)
        nbr_proj = jnp.dot(feat_cols, nbr_rows1, preferred_element_type=jnp.float32)
        part_sum = self_part + slot_total(nbr_proj, ids_all, mask_all) * inv_all
        pre_one = lax.psum_scatter(part_sum, "g", scatter_dimension=0, tiled=True)
        hidden1 = jax.nn.relu(pre_one).astype(jnp.bfloat16)
        mask_bf = mask_local.astype(jnp.bfloat16)
        inv_local = 1.0 / jnp.sum(mask_local.astype(jnp.float32), axis=1, keepdims=True)

        def nbr_average(rows_local):
            rows_all = lax.all_gather(rows_local, "g", tiled=True)
            gathered = jnp.take(rows_all, ids_local, axis=0)
            summed = jnp.einsum("nk,nkh->nh", mask_bf, gathered, preferred_element_type=jnp.float32)
            return (summed * inv_local).astype(jnp.bfloat16)

        mean_one = nbr_average(hidden1)
        pre_two = jnp.dot(hidden1, w_self2, preferred_element_type=jnp.float32) + jnp.dot(mean_one, w_nbr2, preferred_element_type=jnp.float32)
        hidden2 = jax.nn.relu(pre_two).astype(jnp.bfloat16)
        mean_two = nbr_average(hidden2)
        return jnp.dot(hidden2, w_self3, preferred_element_type=jnp.float32) + jnp.dot(mean_two, w_nbr3, preferred_element_type=jnp.float32)

    col_split = P(None, "g")
    row_split = P("g", None)
    replicated = P()
    return jax.shard_map(
        device_step,
        mesh=mesh,
        in_specs=(col_split, row_split, row_split, row_split, row_split, replicated, replicated, replicated, replicated),
        out_specs=row_split,
        check_vma=False,
    )
```

profile of v0, /device:TPU:1, one launch (start us, length us, event | category | flops | bytes accessed | tf_op | source)
XLA Modules:
  0.0 1818.1 jit_solution(6209768636308351995)
XLA Ops:
  6.5 46.1 %all_gather.12 = s32[16384,15]{0,1:T(8,128)S(1)} all-gather(s32[512,15]{0,1:T(8,128)} %param.17), channel_id=1, replica_groups=mesh['g'=32] {'g'}, dimensions={0}, use_global_device_ids=true | all-gather | bytes 1013760 | tf_op jit(solution)/shard_map/all_gather | solution.py:21
  52.6 0.2 convert_reduce_fusion
  52.9 0.6 broadcast_divide_fusion
  53.5 39.5 %all_gather.13 = s32[16384,15]{0,1:T(8,128)S(1)} all-gather(s32[512,15]{0,1:T(8,128)} %param.16), channel_id=1, replica_groups=mesh['g'=32] {'g'}, dimensions={0}, use_global_device_ids=true | all-gather | bytes 1013760 | tf_op jit(solution)/shard_map/all_gather | solution.py:20
  93.0 13.9 fusion.18
  106.9 1283.0 %while.11 = (s32[]{:T(128)}, f32[16384,256]{1,0:T(8,128)}, f32[15,16384]{1,0:T(8,128)S(1)}, s32[15,16384]{1,0:T(8,128)S(1)}, f32[16384,256]{1,0:T(8,128)}, /*index=5*/s32[]{:T(128)}, s32[]{:T(128)}) while((s32[]{:T(128)}, f32[16384,256]{1,0:T(8,128)}, f32[15,16384]{1,0:T(8,128)S(1)}, s32[15,16384]{1,0:T(8,128)S(1)}, ...), condition=%wide.region_1.2_spmd.clone, body=%wide.region_0.0_spmd.clone.sunk | while | flops 16941060 | bytes 84574304 | solution.py:14
  107.0 0.1 compare_select_fusion.4
  107.1 67.7 %gather_fusion = f32[16384,256]{1,0:T(8,128)} fusion(f32[16384,256]{1,0:T(8,128)} %get-tuple-element.117, s32[16384]{0:T(1024)S(1)} %broadcast_clamp_fusion.2), kind=kCustom, calls=%fused_computation.clone.clone.1 | custom fusion | bytes 33619968 | tf_op jit(solution)/shard_map/while/body/eval_jaxpr/jit(_take)/gather | solution.py:10
  174.8 14.6 select_add_fusion.2
  189.5 0.1 compare_select_fusion.4
  189.7 67.7 %gather_fusion = f32[16384,256]{1,0:T(8,128)} fusion(f32[16384,256]{1,0:T(8,128)} %get-tuple-element.117, s32[16384]{0:T(1024)S(1)} %broadcast_clamp_fusion.2), kind=kCustom, calls=%fused_computation.clone.clone.1 | custom fusion | bytes 33619968 | tf_op jit(solution)/shard_map/while/body/eval_jaxpr/jit(_take)/gather | solution.py:10
  257.4 17.8 select_add_fusion.2
  275.3 0.1 compare_select_fusion.4
  275.4 67.7 %gather_fusion = f32[16384,256]{1,0:T(8,128)} fusion(f32[16384,256]{1,0:T(8,128)} %get-tuple-element.117, s32[16384]{0:T(1024)S(1)} %broadcast_clamp_fusion.2), kind=kCustom, calls=%fused_computation.clone.clone.1 | custom fusion | bytes 33619968 | tf_op jit(solution)/shard_map/while/body/eval_jaxpr/jit(_take)/gather | solution.py:10
  343.1 17.8 select_add_fusion.2
  361.0 0.1 compare_select_fusion.4
  361.2 67.7 %gather_fusion = f32[16384,256]{1,0:T(8,128)} fusion(f32[16384,256]{1,0:T(8,128)} %get-tuple-element.117, s32[16384]{0:T(1024)S(1)} %broadcast_clamp_fusion.2), kind=kCustom, calls=%fused_computation.clone.clone.1 | custom fusion | bytes 33619968 | tf_op jit(solution)/shard_map/while/body/eval_jaxpr/jit(_take)/gather | solution.py:10
  428.9 17.8 select_add_fusion.2
  446.8 0.1 compare_select_fusion.4
  446.9 67.7 %gather_fusion = f32[16384,256]{1,0:T(8,128)} fusion(f32[16384,256]{1,0:T(8,128)} %get-tuple-element.117, s32[16384]{0:T(1024)S(1)} %broadcast_clamp_fusion.2), kind=kCustom, calls=%fused_computation.clone.clone.1 | custom fusion | bytes 33619968 | tf_op jit(solution)/shard_map/while/body/eval_jaxpr/jit(_take)/gather | solution.py:10
  514.6 17.8 select_add_fusion.2
  532.5 0.1 compare_select_fusion.4
  532.7 67.7 %gather_fusion = f32[16384,256]{1,0:T(8,128)} fusion(f32[16384,256]{1,0:T(8,128)} %get-tuple-element.117, s32[16384]{0:T(1024)S(1)} %broadcast_clamp_fusion.2), kind=kCustom, calls=%fused_computation.clone.clone.1 | custom fusion | bytes 33619968 | tf_op jit(solution)/shard_map/while/body/eval_jaxpr/jit(_take)/gather | solution.py:10
  600.4 17.8 select_add_fusion.2
  618.3 0.1 compare_select_fusion.4
  618.4 67.7 %gather_fusion = f32[16384,256]{1,0:T(8,128)} fusion(f32[16384,256]{1,0:T(8,128)} %get-tuple-element.117, s32[16384]{0:T(1024)S(1)} %broadcast_clamp_fusion.2), kind=kCustom, calls=%fused_computation.clone.clone.1 | custom fusion | bytes 33619968 | tf_op jit(solution)/shard_map/while/body/eval_jaxpr/jit(_take)/gather | solution.py:10
  686.1 17.8 select_add_fusion.2
  704.0 0.1 compare_select_fusion.4
  704.2 67.7 %gather_fusion = f32[16384,256]{1,0:T(8,128)} fusion(f32[16384,256]{1,0:T(8,128)} %get-tuple-element.117, s32[16384]{0:T(1024)S(1)} %broadcast_clamp_fusion.2), kind=kCustom, calls=%fused_computation.clone.clone.1 | custom fusion | bytes 33619968 | tf_op jit(solution)/shard_map/while/body/eval_jaxpr/jit(_take)/gather | solution.py:10
  771.9 17.8 select_add_fusion.2
  789.9 67.7 %gather_fusion = f32[16384,256]{1,0:T(8,128)} fusion(f32[16384,256]{1,0:T(8,128)} %get-tuple-element.117, s32[16384]{0:T(1024)S(1)} %broadcast_clamp_fusion.2), kind=kCustom, calls=%fused_computation.clone.clone.1 | custom fusion | bytes 33619968 | tf_op jit(solution)/shard_map/while/body/eval_jaxpr/jit(_take)/gather | solution.py:10
  857.6 17.8 select_add_fusion.2
  875.7 67.7 %gather_fusion = f32[16384,256]{1,0:T(8,128)} fusion(f32[16384,256]{1,0:T(8,128)} %get-tuple-element.117, s32[16384]{0:T(1024)S(1)} %broadcast_clamp_fusion.2), kind=kCustom, calls=%fused_computation.clone.clone.1 | custom fusion | bytes 33619968 | tf_op jit(solution)/shard_map/while/body/eval_jaxpr/jit(_take)/gather | solution.py:10
  943.4 17.8 select_add_fusion.2
  961.4 67.7 %gather_fusion = f32[16384,256]{1,0:T(8,128)} fusion(f32[16384,256]{1,0:T(8,128)} %get-tuple-element.117, s32[16384]{0:T(1024)S(1)} %broadcast_clamp_fusion.2), kind=kCustom, calls=%fused_computation.clone.clone.1 | custom fusion | bytes 33619968 | tf_op jit(solution)/shard_map/while/body/eval_jaxpr/jit(_take)/gather | solution.py:10
  1029.1 17.8 select_add_fusion.2
  1047.2 67.7 %gather_fusion = f32[16384,256]{1,0:T(8,128)} fusion(f32[16384,256]{1,0:T(8,128)} %get-tuple-element.117, s32[16384]{0:T(1024)S(1)} %broadcast_clamp_fusion.2), kind=kCustom, calls=%fused_computation.clone.clone.1 | custom fusion | bytes 33619968 | tf_op jit(solution)/shard_map/while/body/eval_jaxpr/jit(_take)/gather | solution.py:10
  1114.9 17.8 select_add_fusion.2
  1132.9 67.7 %gather_fusion = f32[16384,256]{1,0:T(8,128)} fusion(f32[16384,256]{1,0:T(8,128)} %get-tuple-element.117, s32[16384]{0:T(1024)S(1)} %broadcast_clamp_fusion.2), kind=kCustom, calls=%fused_computation.clone.clone.1 | custom fusion | bytes 33619968 | tf_op jit(solution)/shard_map/while/body/eval_jaxpr/jit(_take)/gather | solution.py:10
  1200.6 17.8 select_add_fusion.2
  1218.7 67.7 %gather_fusion = f32[16384,256]{1,0:T(8,128)} fusion(f32[16384,256]{1,0:T(8,128)} %get-tuple-element.117, s32[16384]{0:T(1024)S(1)} %broadcast_clamp_fusion.2), kind=kCustom, calls=%fused_computation.clone.clone.1 | custom fusion | bytes 33619968 | tf_op jit(solution)/shard_map/while/body/eval_jaxpr/jit(_take)/gather | solution.py:10
  1286.4 17.8 select_add_fusion.2
  1304.4 67.7 %gather_fusion = f32[16384,256]{1,0:T(8,128)} fusion(f32[16384,256]{1,0:T(8,128)} %get-tuple-element.117, s32[16384]{0:T(1024)S(1)} %broadcast_clamp_fusion.2), kind=kCustom, calls=%fused_computation.clone.clone.1 | custom fusion | bytes 33619968 | tf_op jit(solution)/shard_map/while/body/eval_jaxpr/jit(_take)/gather | solution.py:10
  1372.1 17.8 select_add_fusion.2
  1390.0 14.8 convolution_add_fusion
  1404.8 180.3 %reduce-scatter.2.cloned.1.call-done = f32[512,256]{1,0:T(8,128)} async-done(((f32[16384,256]{1,0:T(8,128)}), f32[512,256]{1,0:T(8,128)}) %reduce-scatter.2.cloned.1.call-update) | async-done | bytes 524304 | tf_op jit(solution)/shard_map/reduce_scatter | solution.py:26
  1585.1 1.8 maximum_convert_fusion
  1587.0 0.2 all-gather.5.cloned.1.call-start
  1587.2 0.2 copy.12
  1587.4 0.1 copy.13
  1587.6 0.2 reshape.80
  1587.8 0.2 copy.16
  1588.1 1.2 fusion.19
  1589.3 77.2 %all-gather.3.cloned.1.call-done = bf16[16384,256]{1,0:T(8,128)(2,1)} async-done(((bf16[512,256]{1,0:T(8,128)(2,1)}), bf16[16384,256]{1,0:T(8,128)(2,1)}) %all-gather.3.cloned.1.call-update) | async-done | bytes 8388624 | tf_op jit(solution)/shard_map/all_gather | solution.py:32
  1666.5 22.7 %gather_fusion.1 = bf16[7680,256]{1,0:T(8,128)(2,1)} fusion(bf16[16384,256]{1,0:T(8,128)(2,1)} %all-gather.3.cloned.1.call-done, s32[8192]{0:T(1024)S(1)} %pad_clamp_fusion), kind=kCustom, calls=%fused_computation.1.clone | custom fusion | bytes 7895040 | tf_op jit(solution)/shard_map/jit(_take)/gather | solution.py:33
  1689.2 6.8 reshape.83
  1696.0 4.1 fusion.2
  1700.1 1.0 fusion.9
  1701.1 1.1 fusion.20
  1702.2 74.8 %all-gather.5.cloned.1.call-done = bf16[16384,256]{1,0:T(8,128)(2,1)} async-done(((bf16[512,256]{1,0:T(8,128)(2,1)}), bf16[16384,256]{1,0:T(8,128)(2,1)}) %all-gather.5.cloned.1.call-update) | async-done | bytes 8388624 | tf_op jit(solution)/shard_map/all_gather | solution.py:32
  1777.1 22.8 %gather_fusion.2 = bf16[7680,256]{1,0:T(8,128)(2,1)} fusion(bf16[16384,256]{1,0:T(8,128)(2,1)} %all-gather.5.cloned.1.call-done, s32[8192]{0:T(1024)S(1)} %pad_clamp_fusion), kind=kCustom, calls=%fused_computation.2.clone | custom fusion | bytes 7895040 | tf_op jit(solution)/shard_map/jit(_take)/gather | solution.py:33
  1799.8 6.7 reshape.87
  1806.6 4.1 fusion
  1810.7 0.9 convolution_add_fusion.2
  (85 shorter events, 2.3 us)
Async XLA Ops:
  6.5 86.5 %copy-start = (bf16[264,256]{1,0:T(8,128)(2,1)S(1)}, bf16[264,256]{1,0:T(8,128)(2,1)}, u32[]{:S(2)}) copy-start(bf16[264,256]{1,0:T(8,128)(2,1)} %param.15) | copy-start | bytes 405508
  6.5 1578.6 %reduce-scatter.2.cloned.1.call-start = ((), (), s32[]{:S(2)}) async-start(), calls=%async_computation.1 | async-start | bytes 17301504 | tf_op jit(solution)/shard_map/reduce_scatter | solution.py:26
  106.9 1283.0 %copy-start.2 = (f32[16384]{0:T(1024)S(1)}, f32[16384]{0:T(1024)}, u32[]{:S(2)}) copy-start(f32[16384]{0:T(1024)} %broadcast_divide_fusion) | copy-start | bytes 196612
  106.9 1283.0 %copy-start.5 = (bf16[264,256]{1,0:T(8,128)(2,1)S(1)}, bf16[264,256]{1,0:T(8,128)(2,1)}, u32[]{:S(2)}) copy-start(bf16[264,256]{1,0:T(8,128)(2,1)} %param.14) | copy-start | bytes 405508
  1404.7 182.5 %copy-start.3 = (s32[512,15]{0,1:T(8,128)S(1)}, s32[512,15]{0,1:T(8,128)}, u32[]{:S(2)}) copy-start(s32[512,15]{0,1:T(8,128)} %param.16) | copy-start | bytes 92164
  1404.8 183.1 %copy-start.4 = (s32[512,15]{0,1:T(8,128)S(1)}, s32[512,15]{0,1:T(8,128)}, u32[]{:S(2)}) copy-start(s32[512,15]{0,1:T(8,128)} %param.17) | copy-start | bytes 92164
  1404.8 183.3 %copy-start.6 = (bf16[256,256]{1,0:T(8,128)(2,1)S(1)}, bf16[256,256]{1,0:T(8,128)(2,1)}, u32[]{:S(2)}) copy-start(bf16[256,256]{1,0:T(8,128)(2,1)} %param.18) | copy-start | bytes 393220
  1404.8 261.7 %all-gather.3.cloned.1.call-start = ((), (), s32[]{:S(2)}) async-start(), calls=%async_computation.2 | async-start | bytes 8650752 | tf_op jit(solution)/shard_map/all_gather | solution.py:32
  1587.0 190.1 %all-gather.5.cloned.1.call-start = ((), (), s32[]{:S(2)}) async-start(), calls=%async_computation.3 | async-start | bytes 8650752 | tf_op jit(solution)/shard_map/all_gather | solution.py:32
  1689.2 10.9 copy-start.7
  1689.2 11.9 copy-start.8
  1777.1 34.5 %copy-start.1 = (bf16[264,256]{1,0:T(8,128)(2,1)S(1)}, bf16[264,256]{1,0:T(8,128)(2,1)}, u32[]{:S(2)}) copy-start(bf16[264,256]{1,0:T(8,128)(2,1)} %param.15) | copy-start | bytes 405508
  1799.8 10.8 copy-start.9
Sparse Core Ops, SparseCore 0:
  1404.9 180.1 reduce-scatter.1
  1588.0 78.4 all-gather.2
  1701.2 75.7 all-gather.4
where the time goes:
time: 1820 us
  local copies, waits for them, and re-layouts  1080 us (59%)
  waiting for transfers between devices  332 us (18%)
  other arithmetic  269 us (15%)
  blocking collectives  85.5 us (5%)
  matrix products  41 us (2%)
    gather x15, local copies, waits for them, and re-layouts, add_slot(): picked = jnp.take(row_data, ids_col, axis=0).astype(jnp.float32)  1020 us
    add x15, other arithmetic, add_slot(): return (acc_sum + mask_col[:, None] * picked, None)  264 us
    reduce_scatter x1, waiting for transfers between devices, device_step(): pre_one = lax.psum_scatter(part_sum, 'g', scatter_dimension=0, tiled=True)  180 us
    all_gather x2, waiting for transfers between devices, nbr_average(): rows_all = lax.all_gather(rows_local, 'g', tiled=True)  152 us
    gather x4, local copies, waits for them, and re-layouts, nbr_average(): gathered = jnp.take(rows_all, ids_local, axis=0)  59 us
    all_gather x1, blocking collectives, device_step(): mask_all = lax.all_gather(mask_local, 'g', tiled=True).astype(jnp.float32)  46.1 us
    all_gather x1, blocking collectives, device_step(): ids_all = lax.all_gather(ids_local, 'g', tiled=True)  39.5 us
  transfers between devices with their start and end apart: 3, of which 3 were waited for; matrix products, arithmetic and copies ran while one was open for 0% of the time, Pallas kernels for 0%

commit v1 on v0

v1 whole, which is shorter than its diff:
```python
import functools

import jax
import jax.numpy as jnp
from jax import lax
from jax.experimental import pallas as pl
from jax.experimental.pallas import tpu as pltpu
from jax.sharding import PartitionSpec as P

MESH = pl.DeviceIdType.MESH
BF = jnp.bfloat16
F32 = jnp.float32


def place():
    me = lax.axis_index("g")
    core = lax.rem(me, 2)
    x = lax.rem(me // 2, 2)
    y = lax.rem(me // 4, 2)
    z = me // 8
    return me, me + 1 - 2 * core, me + 2 - 4 * x, me + 4 - 8 * y, z


def along_z(dev, z, j):
    return dev + 8 * (lax.rem(z + j, 4) - z)


def greet(peers):
    barrier = pltpu.get_barrier_semaphore()
    for peer in peers:
        pl.semaphore_signal(barrier, inc=1, device_id=(peer,), device_id_type=MESH)
    pl.semaphore_wait(barrier, len(peers))


def remote(src, dst, send_sem, recv_sem, dev):
    return pltpu.make_async_remote_copy(
        src_ref=src, dst_ref=dst, send_sem=send_sem, recv_sem=recv_sem, device_id=(dev,), device_id_type=MESH
    )


STEPS = (2, 1, 3, 0)
DG, XN, YN, ME = range(4)


def scatter_kernel(
    feat, w_ref, nbr_out, self_out,
    own, got, w_got, to_x, to_y, from_x, from_y, to_z, from_z,
    own_sem, gs_sem, gr_sem, w_sem, xs_sem, xr_sem, ys_sem, yr_sem, zs_sem, zr_sem,
):
    me, mate, xn, yn, z = place()
    dg = xn + yn - me
    hid, rows = nbr_out.shape
    greet([mate, xn, yn] + [along_z(me, z, j) for j in (1, 2, 3)])
    mate_shift = mate - me

    w_copy = remote(w_ref, w_got, w_sem.at[0], w_sem.at[1], mate)
    w_copy.start()
    own_copies, mate_copies = [], []
    for t, j in enumerate(STEPS):
        for q, dev in ((DG, dg), (XN, xn), (YN, yn), (ME, me)):
            slot = t * 4 + q
            dest = along_z(dev, z, j)
            a = pltpu.make_async_copy(feat.at[:, pl.ds(pl.multiple_of(dest * rows, rows), rows)], own.at[slot], own_sem.at[slot])
            a.start()
            b = remote(
                feat.at[:, pl.ds(pl.multiple_of((dest + mate_shift) * rows, rows), rows)], got.at[slot],
                gs_sem.at[slot], gr_sem.at[slot], mate,
            )
            b.start()
            own_copies.append(a)
            mate_copies.append(b)

    chunk = 256

    def project(slot, half, r):
        part = pl.ds(half * hid, hid)
        return jnp.dot(w_ref[part, :], own[slot, :, pl.ds(r, chunk)], preferred_element_type=F32) + jnp.dot(
            w_got[part, :], got[slot, :, pl.ds(r, chunk)], preferred_element_type=F32
        )

    def tiles(body):
        def step(i, carry):
            body(pl.multiple_of(i * chunk, chunk))
            return carry

        lax.fori_loop(0, rows // chunk, step, 0)

    def ready(slot):
        own_copies[slot].wait()
        mate_copies[slot].wait_recv()

    copies = {}

    def send_x(t, m):
        c = remote(to_x.at[t, m], from_x.at[t, m], xs_sem.at[t, m], xr_sem.at[t, m], xn)
        c.start()
        copies["x", t, m] = c

    def send_y(t, m):
        c = remote(to_y.at[t, m], from_y.at[t, m], ys_sem.at[t, m], yr_sem.at[t, m], yn)
        c.start()
        copies["y", t, m] = c

    def stage_one(t):
        ready(t * 4 + DG)

        def body(r):
            to_x[t, 0, :, pl.ds(r, chunk)] = project(t * 4 + DG, 0, r).astype(BF)
            to_y[t, 0, :, pl.ds(r, chunk)] = project(t * 4 + DG, 1, r).astype(BF)

        tiles(body)
        send_x(t, 0)
        send_y(t, 0)
        ready(t * 4 + XN)
        ready(t * 4 + YN)

        def body_raw(r):
            to_x[t, 1, :, pl.ds(r, chunk)] = project(t * 4 + XN, 0, r).astype(BF)
            to_y[t, 1, :, pl.ds(r, chunk)] = project(t * 4 + YN, 1, r).astype(BF)

        tiles(body_raw)
        send_x(t, 1)
        send_y(t, 1)

    def stage_relay(t):
        copies["x", t, 0].wait_recv()
        copies["y", t, 0].wait_recv()

        def body(r):
            to_x[t, 2, :, pl.ds(r, chunk)] = (project(t * 4 + XN, 1, r) + from_y[t, 0, :, pl.ds(r, chunk)].astype(F32)).astype(BF)
            to_y[t, 2, :, pl.ds(r, chunk)] = (project(t * 4 + YN, 0, r) + from_x[t, 0, :, pl.ds(r, chunk)].astype(F32)).astype(BF)

        tiles(body)
        send_x(t, 2)
        send_y(t, 2)

    def plane_sum(t, half, r):
        mx, my = (1, 2) if half == 0 else (2, 1)
        return (
            project(t * 4 + ME, half, r)
            + from_x[t, mx, :, pl.ds(r, chunk)].astype(F32)
            + from_y[t, my, :, pl.ds(r, chunk)].astype(F32)
        )

    def plane_ready(t):
        ready(t * 4 + ME)
        for m in (1, 2):
            copies["x", t, m].wait_recv()
            copies["y", t, m].wait_recv()

    def stage_z(t):
        plane_ready(t)
        j = STEPS[t]

        def body(r):
            for half in (0, 1):
                to_z[t, half, :, pl.ds(r, chunk)] = plane_sum(t, half, r).astype(BF)

        tiles(body)
        c = remote(to_z.at[t], from_z.at[3 - j], zs_sem.at[t], zr_sem.at[3 - j], along_z(me, z, j))
        c.start()
        copies["z", t] = c

    w_copy.wait_recv()
    stage_one(0)
    stage_one(1)
    stage_relay(0)
    stage_one(2)
    stage_relay(1)
    stage_z(0)
    stage_one(3)
    stage_relay(2)
    stage_z(1)
    stage_relay(3)
    stage_z(2)
    plane_ready(3)
    for k in range(3):
        remote(to_z.at[k], from_z.at[k], zs_sem.at[k], zr_sem.at[k], me).wait_recv()

    def last(r):
        at = pl.ds(r, chunk)
        total = [
            plane_sum(3, half, r) + from_z[0, half, :, at].astype(F32) + from_z[1, half, :, at].astype(F32) + from_z[2, half, :, at].astype(F32)
            for half in (0, 1)
        ]
        nbr_out[:, at] = total[0].astype(BF)
        self_out[:, at] = total[1]

    tiles(last)
    w_copy.wait_send()
    for c in mate_copies:
        c.wait_send()
    for c in copies.values():
        c.wait_send()


def scatter(feat, weights, rows):
    both, depth = weights.shape
    hid = both // 2
    vmem = pl.BlockSpec(memory_space=pltpu.VMEM)
    dma = pltpu.SemaphoreType.DMA
    return pl.pallas_call(
        scatter_kernel,
        out_shape=(jax.ShapeDtypeStruct((hid, rows), BF), jax.ShapeDtypeStruct((hid, rows), F32)),
        in_specs=[pl.BlockSpec(memory_space=pl.ANY), vmem],
        out_specs=(vmem, vmem),
        scratch_shapes=[
            pltpu.VMEM((16, depth, rows), BF),
            pltpu.VMEM((16, depth, rows), BF),
            pltpu.VMEM((both, depth), BF),
            pltpu.VMEM((4, 3, hid, rows), BF),
            pltpu.VMEM((4, 3, hid, rows), BF),
            pltpu.VMEM((4, 3, hid, rows), BF),
            pltpu.VMEM((4, 3, hid, rows), BF),
            pltpu.VMEM((3, 2, hid, rows), BF),
            pltpu.VMEM((3, 2, hid, rows), BF),
            dma((16,)), dma((16,)), dma((16,)), dma((2,)),
            dma((4, 3)), dma((4, 3)), dma((4, 3)), dma((4, 3)), dma((3,)), dma((3,)),
        ],
        compiler_params=pltpu.CompilerParams(collective_id=0, has_side_effects=True),
        name="scatter",
    )(feat, weights)


def count_kernel(ids, out):
    fan = ids.shape[0]
    tall, wide = out.shape
    base = pl.program_id(0) * tall
    step = 32

    def body(t, carry):
        r = pl.multiple_of(t * step, step)
        node = lax.broadcasted_iota(jnp.int32, (step, wide), 0) + (base + r)
        total = jnp.zeros((step, wide), F32)
        for k in range(fan):
            total = jnp.where(ids[pl.ds(k, 1), :] == node, total + 1.0, total)
        out[pl.ds(r, step), :] = total.astype(BF)
        return carry

    lax.fori_loop(0, tall // step, body, 0)


def count(ids, n):
    fan, rows = ids.shape
    return pl.pallas_call(
        count_kernel,
        grid=(n,),
        out_shape=jax.ShapeDtypeStruct((n, rows, rows), BF),
        in_specs=[pl.BlockSpec((fan, rows), lambda b: (0, 0))],
        out_specs=pl.BlockSpec((None, rows, rows), lambda b: (b, 0, 0)),
        name="count",
    )(ids)


def gather_kernel(layer, *refs):
    counts, mask, rows_in = refs[:3]
    extra = refs[3:4] if layer == 1 else refs[3:5]
    (out, full, edges, total, ed_sem, xs_sem, xr_sem, ys_sem, yr_sem, zs_sem, zr_sem, cs_sem, cr_sem) = refs[3 + len(extra):]
    me, mate, xn, yn, z = place()
    dg = xn + yn - me
    hid, rows = rows_in.shape
    half = hid // 2
    greet([mate, xn, yn] + [along_z(me, z, j) for j in (1, 2, 3)])
    top, bottom = pl.ds(0, half), pl.ds(half, half)
    started = []

    def go(src, dst, send_sem, recv_sem, dev):
        c = remote(src, dst, send_sem, recv_sem, dev)
        c.start()
        started.append(c)

    def arrived(dst, recv_sem, send_sem):
        remote(dst, dst, send_sem, recv_sem, me).wait_recv()

    for j in (1, 3, 2):
        go(rows_in, full.at[me], zs_sem.at[j - 1], zr_sem.at[3 - j], along_z(me, z, j))
    go(rows_in, full.at[me], xs_sem.at[0], xr_sem.at[0], xn)
    go(rows_in, full.at[me], ys_sem.at[0], yr_sem.at[0], yn)
    go(rows_in, full.at[me], cs_sem.at[0], cr_sem.at[0], mate)
    loads = [pltpu.make_async_copy(counts.at[pl.ds(8 * q, 8)], edges.at[pl.ds(8 * q, 8)], ed_sem.at[q]) for q in range(4)]
    for load in loads:
        load.start()
    for load in loads:
        load.wait()

    chunk = 256

    def add(src, b, first=False):
        def body(i, carry):
            at = pl.ds(pl.multiple_of(i * chunk, chunk), chunk)
            part = jnp.dot(src[...], edges[b, :, at], preferred_element_type=F32)
            total[:, at] = part if first else total[:, at] + part
            return carry

        lax.fori_loop(0, rows // chunk, body, 0)

    add(rows_in, me, True)

    def column(j):
        b = along_z(me, z, j)
        arrived(full.at[b], zr_sem.at[j - 1], zs_sem.at[j - 1])
        go(full.at[b], full.at[b], xs_sem.at[j], xr_sem.at[j], xn)
        go(full.at[b], full.at[b], ys_sem.at[j], yr_sem.at[j], yn)
        go(full.at[b], full.at[b], cs_sem.at[j], cr_sem.at[j], mate)
        add(full.at[b], b)

    def relay(j):
        bx, by = along_z(xn, z, j), along_z(yn, z, j)
        arrived(full.at[bx], xr_sem.at[j], xs_sem.at[j])
        go(full.at[bx, top], full.at[bx, top], ys_sem.at[4 + j], yr_sem.at[4 + j], yn)
        go(full.at[bx], full.at[bx], cs_sem.at[4 + j], cr_sem.at[4 + j], mate)
        arrived(full.at[by], yr_sem.at[j], ys_sem.at[j])
        go(full.at[by, bottom], full.at[by, bottom], xs_sem.at[4 + j], xr_sem.at[4 + j], xn)
        go(full.at[by], full.at[by], cs_sem.at[8 + j], cr_sem.at[8 + j], mate)
        add(full.at[bx], bx)
        add(full.at[by], by)

    def diagonal(j):
        b = along_z(dg, z, j)
        arrived(full.at[b, top], yr_sem.at[4 + j], ys_sem.at[4 + j])
        go(full.at[b, top], full.at[b, top], cs_sem.at[12 + j], cr_sem.at[12 + j], mate)
        arrived(full.at[b, bottom], xr_sem.at[4 + j], xs_sem.at[4 + j])
        go(full.at[b, bottom], full.at[b, bottom], cs_sem.at[16 + j], cr_sem.at[16 + j], mate)
        add(full.at[b], b)

    shift = mate - me

    def from_mate(j):
        for k, dev in ((0, me), (4, xn), (8, yn)):
            b = along_z(dev, z, j) + shift
            arrived(full.at[b], cr_sem.at[k + j], cs_sem.at[k + j])
            add(full.at[b], b)

    def from_mate_diagonal(j):
        b = along_z(dg, z, j) + shift
        arrived(full.at[b, top], cr_sem.at[12 + j], cs_sem.at[12 + j])
        arrived(full.at[b, bottom], cr_sem.at[16 + j], cs_sem.at[16 + j])
        add(full.at[b], b)

    column(1)
    column(3)
    relay(0)
    column(2)
    relay(1)
    relay(3)
    diagonal(0)
    relay(2)
    from_mate(0)
    from_mate(1)
    from_mate(3)
    diagonal(1)
    from_mate_diagonal(0)
    diagonal(3)
    from_mate(2)
    from_mate_diagonal(1)
    from_mate_diagonal(3)
    diagonal(2)
    from_mate_diagonal(2)

    mean = total[...] * (1.0 / jnp.sum(mask[...].astype(F32), axis=0, keepdims=True))
    if layer == 1:
        out[...] = jnp.maximum(extra[0][...] + mean, 0.0).astype(BF)
    else:
        w_self, w_nbr = extra
        pre = jnp.dot(w_self[...], rows_in[...], preferred_element_type=F32) + jnp.dot(
            w_nbr[...], mean.astype(BF), preferred_element_type=F32
        )
        out[...] = jnp.maximum(pre, 0.0).astype(BF) if layer == 2 else pre
    for c in started:
        c.wait_send()


def gather(layer, counts, mask, rows_in, *extra):
    hid, rows = rows_in.shape
    n = counts.shape[0]
    vmem = pl.BlockSpec(memory_space=pltpu.VMEM)
    dma = pltpu.SemaphoreType.DMA
    cols = extra[-1].shape[0]
    return pl.pallas_call(
        functools.partial(gather_kernel, layer),
        out_shape=jax.ShapeDtypeStruct((cols, rows), F32 if layer == 3 else BF),
        in_specs=[pl.BlockSpec(memory_space=pl.ANY)] + [vmem] * (2 + len(extra)),
        out_specs=vmem,
        scratch_shapes=[
            pltpu.VMEM((n, hid, rows), BF),
            pltpu.VMEM((n, rows, rows), BF),
            pltpu.VMEM((hid, rows), F32),
            dma((4,)), dma((8,)), dma((8,)), dma((8,)), dma((8,)), dma((3,)), dma((3,)), dma((20,)), dma((20,)),
        ],
        compiler_params=pltpu.CompilerParams(collective_id=layer, has_side_effects=True),
        name=f"gather{layer}",
    )(counts, mask, rows_in, *extra)


def solution(mesh):
    def device_step(feat, w_self1, w_nbr1, ids, mask, w_self2, w_nbr2, w_self3, w_nbr3):
        rows = ids.shape[0]
        mask = mask.T
        listed = jnp.where(mask > 0, ids.T, -1)
        counts = count(listed, feat.shape[0] // rows)
        nbr1, self1 = scatter(feat.T, jnp.concatenate([w_nbr1.T, w_self1.T], axis=0), rows)
        hidden1 = gather(1, counts, mask, nbr1, self1)
        hidden2 = gather(2, counts, mask, hidden1, w_self2.T, w_nbr2.T)
        return gather(3, counts, mask, hidden2, w_self3.T, w_nbr3.T).T

    col_split, row_split, replicated = P(None, "g"), P("g", None), P()
    return jax.shard_map(
        device_step,
        mesh=mesh,
        in_specs=(col_split, row_split, row_split, row_split, row_split, replicated, replicated, replicated, replicated),
        out_specs=row_split,
        check_vma=False,
    )
```

time: 1820 us -> 307 us (0.17)
  local copies, waits for them, and re-layouts: 1080 us -> 3.18 us
  waiting for transfers between devices: 332 us -> 0 us
  Pallas kernels: 0 us -> 301 us
  other arithmetic: 269 us -> 2.22 us
  blocking collectives: 85.5 us -> 0 us
  matrix products: 41 us -> 0 us
    gather x19 -> x0, local copies, waits for them, and re-layouts: 1070 us -> none  [the longest x15 1020 us: add_slot(): picked = jnp.take(row_data, ids_col, axis=0).astype(jnp.float32)]
    pallas_call x0 -> x5, Pallas kernels: none -> 301 us  [the longest x3 156 us: gather(): pl.pallas_call(functools.partial(gather_kernel, layer), out_shape=jax.Sha...]
    add x15 -> x0, other arithmetic: 264 us -> none  [add_slot(): return (acc_sum + mask_col[:, None] * picked, None)]
    reduce_scatter x1 -> x0, waiting for transfers between devices: 180 us -> none  [device_step(): pre_one = lax.psum_scatter(part_sum, 'g', scatter_dimension=0, tiled=True)]
    all_gather x2 -> x0, waiting for transfers between devices: 152 us -> none  [nbr_average(): rows_all = lax.all_gather(rows_local, 'g', tiled=True)]
    all_gather x2 -> x0, blocking collectives: 85.5 us -> none  [the longest x1 46.1 us: device_step(): mask_all = lax.all_gather(mask_local, 'g', tiled=True).astype(jnp.float32)]
    dot_general x8 -> x0, matrix products: 41 us -> none  [the longest x1 14.8 us: device_step(): jnp.dot(feat_cols, self_rows1, preferred_element_type=jnp.float32)]
  transfers between devices with their start and end apart: 3 -> 0, of which waited for: 3 -> 0; matrix products, arithmetic and copies ran while one was open for 0% -> 0% of each run, Pallas kernels for 0% -> 0%
where the time goes in v1:
time: 307 us
  Pallas kernels  301 us (98%)
  local copies, waits for them, and re-layouts  3.18 us (1%)
    pallas_call x3, Pallas kernels, gather(): pl.pallas_call(functools.partial(gather_kernel, layer), out_shape=jax.Sha...  156 us
    pallas_call x1, Pallas kernels, scatter(): pl.pallas_call(scatter_kernel, out_shape=(jax.ShapeDtypeStruct((hid, rows...  89.6 us
    pallas_call x1, Pallas kernels, count(): pl.pallas_call(count_kernel, grid=(n,), out_shape=jax.ShapeDtypeStruct((n...  56.1 us

profile of v1, /device:TPU:1, one launch (start us, length us, event | category | flops | bytes accessed | tf_op | source)
XLA Modules:
  0.0 306.9 jit_solution(10197555244142224761)
XLA Ops:
  0.0 0.0 copy-start
  0.0 0.0 copy-start.1
  0.0 1.4 bitcast_select_fusion.ids
  1.4 56.1 %count.1.refs_0_ = bf16[32,512,512]{2,1,0:T(8,128)(2,1)} custom-call(s32[15,512]{1,0:T(8,128)} %bitcast_select_fusion.ids), custom_call_target="tpu_custom_call" | custom-call | tf_op jit(solution)/shard_map/count/pallas_call | solution.py:245
  57.5 0.0 copy-start.2
  57.5 0.0 copy-start.3
  57.5 0.0 copy-done
  57.5 0.2 copy.10
  57.7 0.0 copy-done.1
  57.7 0.2 copy.11
  57.9 0.8 pad_maximum_fusion.w_ref
  58.7 89.6 %scatter.1 = (bf16[256,512]{1,0:T(8,128)(2,1)}, f32[256,512]{1,0:T(8,128)}) custom-call(bf16[264,16384]{1,0:T(8,128)(2,1)} %bitcast.12, bf16[512,264]{1,0:T(8,128)(2,1)} %pad_maximum_fusion.w_ref), custom_call_target="tpu_custom_call" | custom-call | tf_op jit(solution)/shard_map/scatter/pallas_call | solution.py:202
  148.3 51.6 %gather1.1.refs_2_ = bf16[256,512]{1,0:T(8,128)(2,1)} custom-call(bf16[32,512,512]{2,1,0:T(8,128)(2,1)} %count.1.refs_0_, s32[15,512]{1,0:T(8,128)} %bitcast.15, bf16[256,512]{1,0:T(8,128)(2,1)} %get-tuple-element.7.refs_2_, f32[256,512]{1,0:T(8,128)} %get-tuple-element.8.refs_3_), custom_call_target="tpu_custom_call" | custom-call | tf_op jit(solution)/shard_map/gather1/pallas_call | solution.py:379
  199.9 0.0 copy-done.2
  199.9 0.8 copy.12
  200.7 0.0 copy-done.3
  200.7 0.8 copy.13
  201.4 53.6 %gather2.1.refs_2_ = bf16[256,512]{1,0:T(8,128)(2,1)} custom-call(bf16[32,512,512]{2,1,0:T(8,128)(2,1)} %count.1.refs_0_, s32[15,512]{1,0:T(8,128)} %bitcast.16, bf16[256,512]{1,0:T(8,128)(2,1)} %gather1.1.refs_2_, bf16[256,256]{1,0:T(8,128)(2,1)} %bitcast.18, bf16[256,256]{1,0:T(8,128)(2,1)} %bitcast.19), custom_call_target="tpu_custom_call" | custom-call | tf_op jit(solution)/shard_map/gather2/pallas_call | solution.py:379
  255.0 50.6 %gather3.1 = f32[5,512]{1,0:T(8,128)} custom-call(bf16[32,512,512]{2,1,0:T(8,128)(2,1)} %count.1.refs_0_, s32[15,512]{1,0:T(8,128)} %bitcast.17, bf16[256,512]{1,0:T(8,128)(2,1)} %gather2.1.refs_2_, bf16[5,256]{1,0:T(8,128)(2,1)} %bitcast.21, bf16[5,256]{1,0:T(8,128)(2,1)} %bitcast.22), custom_call_target="tpu_custom_call" | custom-call | tf_op jit(solution)/shard_map/gather3/pallas_call | solution.py:379
  305.6 1.3 copy.15
Async XLA Ops:
  0.0 57.5 %copy-start = (bf16[264,256]{1,0:T(8,128)(2,1)S(1)}, bf16[264,256]{1,0:T(8,128)(2,1)}, u32[]{:S(2)}) copy-start(bf16[264,256]{1,0:T(8,128)(2,1)} %param.11) | copy-start | bytes 405508
  0.0 57.7 %copy-start.1 = (bf16[264,256]{1,0:T(8,128)(2,1)S(1)}, bf16[264,256]{1,0:T(8,128)(2,1)}, u32[]{:S(2)}) copy-start(bf16[264,256]{1,0:T(8,128)(2,1)} %param.10) | copy-start | bytes 405508
  57.5 142.4 %copy-start.2 = (bf16[256,256]{1,0:T(8,128)(2,1)S(1)}, bf16[256,256]{1,0:T(8,128)(2,1)}, u32[]{:S(2)}) copy-start(bf16[256,256]{1,0:T(8,128)(2,1)} %param.14) | copy-start | bytes 393220
  57.5 143.1 %copy-start.3 = (bf16[256,256]{1,0:T(8,128)(2,1)S(1)}, bf16[256,256]{1,0:T(8,128)(2,1)}, u32[]{:S(2)}) copy-start(bf16[256,256]{1,0:T(8,128)(2,1)} %param.15) | copy-start | bytes 393220

commit v2 on v0

v2 whole, which is shorter than its diff:
```python
import jax
import jax.numpy as jnp
from jax import lax
from jax.experimental import pallas as pl
from jax.experimental.pallas import tpu as pltpu
from jax.sharding import PartitionSpec as P

MESH = pl.DeviceIdType.MESH
BF = jnp.bfloat16
F32 = jnp.float32
DG, XN, YN, ME = range(4)


def remote(src, dst, send_sem, recv_sem, dev):
    return pltpu.make_async_remote_copy(
        src_ref=src, dst_ref=dst, send_sem=send_sem, recv_sem=recv_sem, device_id=(dev,), device_id_type=MESH
    )


def kernel(
    feat, w_ref, ids, mask, w_self2, w_nbr2, w_self3, w_nbr3, out,
    own, got, w_got, to_x, to_y, from_x, from_y, to_z, from_z, listed, edges, full, total, self1, hidden,
    own_sem, gs_sem, gr_sem, w_sem, sxs_sem, sxr_sem, sys_sem, syr_sem, szs_sem, szr_sem,
    xs_sem, xr_sem, ys_sem, yr_sem, zs_sem, zr_sem, cs_sem, cr_sem,
):
    me = lax.axis_index("g")
    core = lax.rem(me, 2)
    x = lax.rem(me // 2, 2)
    y = lax.rem(me // 4, 2)
    z = me // 8
    mate, xn, yn = me + 1 - 2 * core, me + 2 - 4 * x, me + 4 - 8 * y
    dg = xn + yn - me
    f = (z * (3 - z)) // 2
    inner = f == 1
    across, beyond = 3 - z, z + 2 - 4 * (z // 2)
    planes = (z, z + 1 - 2 * lax.rem(z, 2), f * across + (1 - f) * beyond, f * beyond + (1 - f) * across)

    def at_plane(dev, k):
        return dev + 8 * (planes[k] - z)

    pair = at_plane(me, 1)
    facing = me + 8 * (across - z)
    hid, rows = self1.shape
    half = hid // 2
    chunk = 256

    barrier = pltpu.get_barrier_semaphore()
    for peer in (mate, xn, yn, pair, facing):
        pl.semaphore_signal(barrier, inc=1, device_id=(peer,), device_id_type=MESH)
    pl.semaphore_wait(barrier, 5)

    def tiles(body):
        def step(i, carry):
            body(pl.ds(pl.multiple_of(i * chunk, chunk), chunk))
            return carry

        lax.fori_loop(0, rows // chunk, step, 0)


    w_copy = remote(w_ref, w_got, w_sem.at[0], w_sem.at[1], mate)
    w_copy.start()
    own_copies, mate_copies = {}, {}
    mate_shift = mate - me

    def fetch(t):
        for q, dev in ((DG, dg), (XN, xn), (YN, yn), (ME, me)):
            slot = t * 4 + q
            dest = at_plane(dev, 3 - t)
            a = pltpu.make_async_copy(
                feat.at[:, pl.ds(pl.multiple_of(dest * rows, rows), rows)], own.at[slot], own_sem.at[slot]
            )
            a.start()
            b = remote(
                feat.at[:, pl.ds(pl.multiple_of((dest + mate_shift) * rows, rows), rows)],
                got.at[slot], gs_sem.at[slot], gr_sem.at[slot], mate,
            )
            b.start()
            own_copies[slot], mate_copies[slot] = a, b

    def ready(slot):
        own_copies[slot].wait()
        mate_copies[slot].wait_recv()

    def project(slot, part, at):
        of = pl.ds(part * hid, hid)
        return jnp.dot(w_ref[of, :], own[slot, :, at], preferred_element_type=F32) + jnp.dot(
            w_got[of, :], got[slot, :, at], preferred_element_type=F32
        )

    copies = {}

    def send_plane(t, m):
        for name, src, dst, ss, rs, dev in (
            ("x", to_x, from_x, sxs_sem, sxr_sem, xn), ("y", to_y, from_y, sys_sem, syr_sem, yn),
        ):
            c = remote(src.at[t, m], dst.at[t, m], ss.at[t, m], rs.at[t, m], dev)
            c.start()
            copies[name, t, m] = c

    def received(t, m):
        copies["x", t, m].wait_recv()
        copies["y", t, m].wait_recv()

    def diagonal_out(t):
        ready(t * 4 + DG)

        def body(at):
            to_x[t, 0, :, at] = project(t * 4 + DG, 0, at).astype(BF)
            to_y[t, 0, :, at] = project(t * 4 + DG, 1, at).astype(BF)

        tiles(body)
        send_plane(t, 0)

    def raw_out(t):
        ready(t * 4 + XN)
        ready(t * 4 + YN)

        def body(at):
            to_x[t, 1, :, at] = project(t * 4 + XN, 0, at).astype(BF)
            to_y[t, 1, :, at] = project(t * 4 + YN, 1, at).astype(BF)

        tiles(body)
        send_plane(t, 1)

    def relay_out(t):
        received(t, 0)

        def body(at):
            to_x[t, 2, :, at] = (project(t * 4 + XN, 1, at) + from_y[t, 0, :, at].astype(F32)).astype(BF)
            to_y[t, 2, :, at] = (project(t * 4 + YN, 0, at) + from_x[t, 0, :, at].astype(F32)).astype(BF)

        tiles(body)
        send_plane(t, 2)

    def plane_sum(t, part, at):
        mx, my = (1, 2) if part == 0 else (2, 1)
        return project(t * 4 + ME, part, at) + from_x[t, mx, :, at].astype(F32) + from_y[t, my, :, at].astype(F32)

    def plane_ready(t):
        ready(t * 4 + ME)
        received(t, 1)
        received(t, 2)

    def z_copy(t, slot, dev):
        return remote(to_z.at[t], from_z.at[slot], szs_sem.at[t], szr_sem.at[slot], dev)

    def z_arrived(slot):
        z_copy(0, slot, pair).wait_recv()

    def z_fill(t, slots):
        def body(at):
            for part in (0, 1):
                v = plane_sum(t, part, at)
                for slot in slots:
                    v = v + from_z[slot, part, :, at].astype(F32)
                to_z[t, part, :, at] = v.astype(BF)

        tiles(body)

    def outer_send(t, slot):
        @pl.when(jnp.logical_not(inner))
        def _():
            z_fill(t, ())
            z_copy(t, slot, pair).start()

    def inner_send(t, add, slot, dev):
        @pl.when(inner)
        def _():
            z_arrived(add)
            z_fill(t, (add,))
            z_copy(t, slot, dev).start()


    listed[...] = jnp.where(mask[...] > 0, ids[...], -1)
    fan = ids.shape[0]
    tall = 128
    next_block = [0]

    def count(blocks):
        first = next_block[0]
        next_block[0] = first + blocks

        def body(i, carry):
            b = i // (rows // tall)
            r = pl.multiple_of(lax.rem(i, rows // tall) * tall, tall)
            base = b * rows + r
            node = lax.broadcasted_iota(jnp.int32, (tall, rows), 0).astype(BF)
            one, zero = jnp.ones((tall, rows), BF), jnp.zeros((tall, rows), BF)
            acc = zero
            for k in range(fan):
                rel = listed[pl.ds(k, 1), :] - base
                rel = jnp.where((rel >= 0) & (rel < tall), rel, -1).astype(F32)
                rel = jnp.broadcast_to(rel, (tall, rows)).astype(BF)
                acc = acc + jnp.where(rel == node, one, zero)
            edges[b, pl.ds(r, tall), :] = acc
            return carry

        lax.fori_loop(first * (rows // tall), (first + blocks) * (rows // tall), body, 0)

    fetch(0)
    w_copy.wait_recv()
    diagonal_out(0)
    raw_out(0)
    fetch(1)
    diagonal_out(1)
    fetch(2)
    fetch(3)
    count(3)
    relay_out(0)
    raw_out(1)
    diagonal_out(2)
    count(5)
    relay_out(1)
    raw_out(2)
    count(4)
    plane_ready(0)
    outer_send(0, 0)
    count(5)
    relay_out(2)
    diagonal_out(3)
    raw_out(3)
    count(2)
    inner_send(0, 0, 2, facing)
    count(3)
    plane_ready(1)
    outer_send(1, 1)
    count(5)
    plane_ready(2)
    outer_send(2, 4)
    inner_send(2, 2, 4, pair)
    inner_send(1, 1, 3, facing)
    count(2)
    relay_out(3)
    count(3)
    plane_ready(3)
    z_arrived(4)

    def last(at):
        hidden[0, :, at] = (plane_sum(3, 0, at) + from_z[4, 0, :, at].astype(F32)).astype(BF)
        self1[:, at] = plane_sum(3, 1, at) + from_z[4, 1, :, at].astype(F32)

    def last_inner(at):
        hidden[0, :, at] = (plane_sum(3, 0, at) + from_z[4, 0, :, at].astype(F32) + from_z[3, 0, :, at].astype(F32)).astype(BF)
        self1[:, at] = plane_sum(3, 1, at) + from_z[4, 1, :, at].astype(F32) + from_z[3, 1, :, at].astype(F32)

    @pl.when(jnp.logical_not(inner))
    def _():
        tiles(last)

    @pl.when(inner)
    def _():
        z_arrived(3)
        tiles(last_inner)

    def finish_scatter():
        w_copy.wait_send()
        for c in mate_copies.values():
            c.wait_send()
        for c in copies.values():
            c.wait_send()
        for t in range(3):
            z_copy(t, 0, pair).wait_send()


    top, bottom = pl.ds(0, half), pl.ds(half, half)

    def average(src, p, after_start):
        started = []

        def go(a, b, send_sem, recv_sem, dev):
            c = remote(a, b, send_sem, recv_sem, dev)
            c.start()
            started.append(c)

        def block(b):
            return full.at[p, b]

        def arrived(dst, recv_sem):
            remote(dst, dst, xs_sem.at[p, 0], recv_sem, mate).wait_recv()

        def add(ref, b, first=False):
            def body(at):
                part = jnp.dot(ref[...], edges[b, :, at], preferred_element_type=F32)
                total[:, at] = part if first else total[:, at] + part

            tiles(body)

        def hop(k, a, b, slot, dev):
            c = remote(a, b, zs_sem.at[p, k], zr_sem.at[p, slot - 1], dev)

            @pl.when(inner)
            def _():
                c.start()

            return c

        go(src, block(me), zs_sem.at[p, 0], zr_sem.at[p, 0], pair)
        hops = [hop(1, src, block(me), 2, facing)]
        go(src, block(me), xs_sem.at[p, 0], xr_sem.at[p, 0], xn)
        go(src, block(me), ys_sem.at[p, 0], yr_sem.at[p, 0], yn)
        go(src, block(me), cs_sem.at[p, 0], cr_sem.at[p, 0], mate)
        after_start()
        add(src, me, True)

        def column(k):
            b = at_plane(me, k)
            arrived(block(b), zr_sem.at[p, k - 1])
            if k == 1:
                hops.append(hop(2, block(b), block(b), 3, facing))
            else:
                hops.append(hop(k + 1, block(b), block(b), k, pair))
            go(block(b), block(b), xs_sem.at[p, k], xr_sem.at[p, k], xn)
            go(block(b), block(b), ys_sem.at[p, k], yr_sem.at[p, k], yn)
            go(block(b), block(b), cs_sem.at[p, k], cr_sem.at[p, k], mate)
            add(block(b), b)

        def relay(k):
            bx, by = at_plane(xn, k), at_plane(yn, k)
            arrived(block(bx), xr_sem.at[p, k])
            go(full.at[p, bx, top], full.at[p, bx, top], ys_sem.at[p, 4 + k], yr_sem.at[p, 4 + k], yn)
            arrived(block(by), yr_sem.at[p, k])
            go(full.at[p, by, bottom], full.at[p, by, bottom], xs_sem.at[p, 4 + k], xr_sem.at[p, 4 + k], xn)
            go(block(bx), block(bx), cs_sem.at[p, 4 + k], cr_sem.at[p, 4 + k], mate)
            go(block(by), block(by), cs_sem.at[p, 8 + k], cr_sem.at[p, 8 + k], mate)
            add(block(bx), bx)
            add(block(by), by)

        def diagonal(k):
            b = at_plane(dg, k)
            arrived(full.at[p, b, top], yr_sem.at[p, 4 + k])
            go(full.at[p, b, top], full.at[p, b, top], cs_sem.at[p, 12 + k], cr_sem.at[p, 12 + k], mate)
            arrived(full.at[p, b, bottom], xr_sem.at[p, 4 + k])
            go(full.at[p, b, bottom], full.at[p, b, bottom], cs_sem.at[p, 16 + k], cr_sem.at[p, 16 + k], mate)
            add(block(b), b)

        def from_mate(k):
            for q, dev in ((0, me), (4, xn), (8, yn)):
                b = at_plane(dev, k) + mate_shift
                arrived(block(b), cr_sem.at[p, q + k])
                add(block(b), b)

        def from_mate_diagonal(k):
            b = at_plane(dg, k) + mate_shift
            arrived(full.at[p, b, top], cr_sem.at[p, 12 + k])
            arrived(full.at[p, b, bottom], cr_sem.at[p, 16 + k])
            add(block(b), b)

        column(1)
        relay(0)
        column(2)
        relay(1)
        column(3)
        from_mate(0)
        diagonal(0)
        relay(2)
        from_mate(1)
        diagonal(1)
        from_mate_diagonal(0)
        relay(3)
        from_mate(2)
        from_mate_diagonal(1)
        diagonal(2)
        from_mate(3)
        from_mate_diagonal(2)
        diagonal(3)
        from_mate_diagonal(3)

        def finish():
            for c in started:
                c.wait_send()

            @pl.when(inner)
            def _():
                for c in hops:
                    c.wait_send()

        return finish

    def mean():
        return total[...] * (1.0 / jnp.sum(mask[...].astype(F32), axis=0, keepdims=True))

    def across_rows(w, v):
        return lax.dot_general(w[...], v, (((0,), (0,)), ((), ())), preferred_element_type=F32)

    finish = average(hidden.at[0], 0, finish_scatter)
    hidden[1] = jnp.maximum(self1[...] + mean(), 0.0).astype(BF)
    finish()
    finish = average(hidden.at[1], 1, lambda: None)
    hidden[2] = jnp.maximum(across_rows(w_self2, hidden[1]) + across_rows(w_nbr2, mean().astype(BF)), 0.0).astype(BF)
    finish()
    finish = average(hidden.at[2], 0, lambda: None)
    out[...] = jnp.dot(w_self3[...], hidden[2], preferred_element_type=F32) + jnp.dot(
        w_nbr3[...], mean().astype(BF), preferred_element_type=F32
    )
    finish()


def solution(mesh):
    def device_step(feat, w_self1, w_nbr1, ids, mask, w_self2, w_nbr2, w_self3, w_nbr3):
        rows, fan = ids.shape
        nodes, depth = feat.shape
        n = nodes // rows
        hid, classes = w_self3.shape
        vmem = pl.BlockSpec(memory_space=pltpu.VMEM)
        dma = pltpu.SemaphoreType.DMA
        logits = pl.pallas_call(
            kernel,
            out_shape=jax.ShapeDtypeStruct((classes, rows), F32),
            in_specs=[pl.BlockSpec(memory_space=pl.ANY)] + [vmem] * 7,
            out_specs=vmem,
            scratch_shapes=[
                pltpu.VMEM((16, depth, rows), BF),
                pltpu.VMEM((16, depth, rows), BF),
                pltpu.VMEM((2 * hid, depth), BF),
                pltpu.VMEM((4, 3, hid, rows), BF),
                pltpu.VMEM((4, 3, hid, rows), BF),
                pltpu.VMEM((4, 3, hid, rows), BF),
                pltpu.VMEM((4, 3, hid, rows), BF),
                pltpu.VMEM((3, 2, hid, rows), BF),
                pltpu.VMEM((5, 2, hid, rows), BF),
                pltpu.VMEM((fan, rows), jnp.int32),
                pltpu.VMEM((n, rows, rows), BF),
                pltpu.VMEM((2, n, hid, rows), BF),
                pltpu.VMEM((hid, rows), F32),
                pltpu.VMEM((hid, rows), F32),
                pltpu.VMEM((3, hid, rows), BF),
                dma((16,)), dma((16,)), dma((16,)), dma((2,)),
                dma((4, 3)), dma((4, 3)), dma((4, 3)), dma((4, 3)), dma((3,)), dma((5,)),
                dma((2, 8)), dma((2, 8)), dma((2, 8)), dma((2, 8)), dma((2, 5)), dma((2, 3)), dma((2, 20)), dma((2, 20)),
            ],
            compiler_params=pltpu.CompilerParams(collective_id=0, has_side_effects=True, vmem_limit_bytes=67043328),
            name="sage",
        )(feat.T, jnp.concatenate([w_nbr1.T, w_self1.T], axis=0), ids.T, mask.T, w_self2, w_nbr2, w_self3.T, w_nbr3.T)
        return logits.T

    col_split, row_split, replicated = P(None, "g"), P("g", None), P()
    return jax.shard_map(
        device_step,
        mesh=mesh,
        in_specs=(col_split, row_split, row_split, row_split, row_split, replicated, replicated, replicated, replicated),
        out_specs=row_split,
        check_vma=False,
    )
```

time: 1820 us -> 207 us (0.11)
  local copies, waits for them, and re-layouts: 1080 us -> 3.47 us
  waiting for transfers between devices: 332 us -> 0 us
  other arithmetic: 269 us -> 0.78 us
  Pallas kernels: 0 us -> 203 us
  blocking collectives: 85.5 us -> 0 us
  matrix products: 41 us -> 0 us
    gather x19 -> x0, local copies, waits for them, and re-layouts: 1070 us -> none  [the longest x15 1020 us: add_slot(): picked = jnp.take(row_data, ids_col, axis=0).astype(jnp.float32)]
    add x15 -> x0, other arithmetic: 264 us -> none  [add_slot(): return (acc_sum + mask_col[:, None] * picked, None)]
    pallas_call x0 -> x1, Pallas kernels: none -> 203 us  [device_step(): pl.pallas_call(kernel, out_shape=jax.ShapeDtypeStruct((classes, rows), F3...]
    reduce_scatter x1 -> x0, waiting for transfers between devices: 180 us -> none  [device_step(): pre_one = lax.psum_scatter(part_sum, 'g', scatter_dimension=0, tiled=True)]
    all_gather x2 -> x0, waiting for transfers between devices: 152 us -> none  [nbr_average(): rows_all = lax.all_gather(rows_local, 'g', tiled=True)]
    all_gather x2 -> x0, blocking collectives: 85.5 us -> none  [the longest x1 46.1 us: device_step(): mask_all = lax.all_gather(mask_local, 'g', tiled=True).astype(jnp.float32)]
    dot_general x8 -> x0, matrix products: 41 us -> none  [the longest x1 14.8 us: device_step(): jnp.dot(feat_cols, self_rows1, preferred_element_type=jnp.float32)]
  transfers between devices with their start and end apart: 3 -> 0, of which waited for: 3 -> 0; matrix products, arithmetic and copies ran while one was open for 0% -> 0% of each run, Pallas kernels for 0% -> 0%
where the time goes in v2:
time: 207 us
  Pallas kernels  203 us (98%)
  local copies, waits for them, and re-layouts  3.47 us (2%)
    pallas_call x1, Pallas kernels, device_step(): pl.pallas_call(kernel, out_shape=jax.ShapeDtypeStruct((classes, rows), F3...  203 us

profile of v2, /device:TPU:1, one launch (start us, length us, event | category | flops | bytes accessed | tf_op | source)
XLA Modules:
  0.0 207.1 jit_solution(8830744048687986864)
XLA Ops:
  0.0 1.1 copy.11
  1.1 1.1 copy.10
  2.2 0.8 pad_maximum_fusion.w_ref
  2.9 202.9 %sage.1 = f32[5,512]{1,0:T(8,128)} custom-call(bf16[264,16384]{1,0:T(8,128)(2,1)} %bitcast.8, bf16[512,264]{1,0:T(8,128)(2,1)} %pad_maximum_fusion.w_ref, s32[15,512]{1,0:T(8,128)} %bitcast.12, s32[15,512]{1,0:T(8,128)} %bitcast.13, bf16[256,256]{1,0:T(8,128)(2,1)} %w_self2.1, bf16[256,256]{1,0:T(8,128)(2,1)} %w_nbr2.1, bf16[5,256]{1,0:T(8,128)(2,1)} %bitcast.14, ...), custom_call_target="tpu_custom_call" | custom-call | tf_op jit(solution)/shard_map/sage/pallas_call | solution.py:406
  205.8 1.3 copy.13

commit v3 on v2

v3 whole, which is shorter than its diff:
```python
import jax
import jax.numpy as jnp
from jax import lax
from jax.experimental import pallas as pl
from jax.experimental.pallas import tpu as pltpu
from jax.sharding import PartitionSpec as P

MESH = pl.DeviceIdType.MESH
BF = jnp.bfloat16
F32 = jnp.float32
DG, XN, YN, ME = range(4)


def remote(src, dst, send_sem, recv_sem, dev):
    return pltpu.make_async_remote_copy(
        src_ref=src, dst_ref=dst, send_sem=send_sem, recv_sem=recv_sem, device_id=(dev,), device_id_type=MESH
    )


def kernel(
    feat, w_ref, ids, mask, w_self2, w_nbr2, w_self3, w_nbr3, out,
    own, got, w_got, to_x, to_y, from_x, from_y, to_z, from_z, to_e, from_e, ends_sum, listed, edges, full, total, self1,
    own_sem, gs_sem, gr_sem, w_sem, sxs_sem, sxr_sem, sys_sem, syr_sem, szs_sem, szr_sem, es_sem, er_sem,
    xs_sem, xr_sem, ys_sem, yr_sem, zs_sem, zr_sem, cs_sem, cr_sem,
):
    me = lax.axis_index("g")
    core = lax.rem(me, 2)
    x = lax.rem(me // 2, 2)
    y = lax.rem(me // 4, 2)
    z = me // 8
    spot = y * 2 + x
    mate, xn, yn = me + 1 - 2 * core, me + 2 - 4 * x, me + 4 - 8 * y
    dg = xn + yn - me
    f = (z * (3 - z)) // 2
    inner = f == 1
    across, beyond = 3 - z, z + 2 - 4 * (z // 2)
    planes = (z, z + 1 - 2 * lax.rem(z, 2), f * across + (1 - f) * beyond, f * beyond + (1 - f) * across)

    def at_plane(dev, k):
        return dev + 8 * (planes[k] - z)

    pair = at_plane(me, 1)
    facing = me + 8 * (across - z)
    hid, rows = self1.shape
    tail = 32
    early, late = hid - tail, tail
    main, ends = pl.ds(0, early), pl.ds(early, late)
    chunk = 256

    barrier = pltpu.get_barrier_semaphore()
    for peer in (mate, xn, yn, pair, facing):
        pl.semaphore_signal(barrier, inc=1, device_id=(peer,), device_id_type=MESH)
    pl.semaphore_wait(barrier, 5)

    def tiles(body):
        def step(i, carry):
            body(pl.ds(pl.multiple_of(i * chunk, chunk), chunk))
            return carry

        lax.fori_loop(0, rows // chunk, step, 0)


    w_copy = remote(w_ref, w_got, w_sem.at[0], w_sem.at[1], mate)
    w_copy.start()
    own_copies, mate_copies = {}, {}
    mate_shift = mate - me

    def fetch(t):
        for q, dev in ((DG, dg), (XN, xn), (YN, yn), (ME, me)):
            slot = t * 4 + q
            dest = at_plane(dev, 3 - t)
            a = pltpu.make_async_copy(
                feat.at[:, pl.ds(pl.multiple_of(dest * rows, rows), rows)], own.at[slot], own_sem.at[slot]
            )
            a.start()
            b = remote(
                feat.at[:, pl.ds(pl.multiple_of((dest + mate_shift) * rows, rows), rows)],
                got.at[slot], gs_sem.at[slot], gr_sem.at[slot], mate,
            )
            b.start()
            own_copies[slot], mate_copies[slot] = a, b

    waited = set()

    def ready(slot):
        if slot in waited:
            return
        waited.add(slot)
        own_copies[slot].wait()
        mate_copies[slot].wait_recv()

    def project(slot, part, at, of=None):
        of = pl.ds(part * hid, early if slot < 12 else hid) if of is None else of
        return jnp.dot(w_ref[of, :], own[slot, :, at], preferred_element_type=F32) + jnp.dot(
            w_got[of, :], got[slot, :, at], preferred_element_type=F32
        )

    copies = {}

    def span(t):
        return main if t < 3 else pl.ds(0, hid)

    def keep(ref, t, m, at, v, q, part):
        ref[t, m, main, at] = v[:early].astype(BF)
        if t == 3:
            ref[t, m, ends, at] = (v[early:] + ends_sum[q, pl.ds(part * late, late), at]).astype(BF)

    def send_plane(t, m):
        for name, src, dst, ss, rs, dev in (
            ("x", to_x, from_x, sxs_sem, sxr_sem, xn), ("y", to_y, from_y, sys_sem, syr_sem, yn),
        ):
            c = remote(src.at[t, m, span(t)], dst.at[t, m, span(t)], ss.at[t, m], rs.at[t, m], dev)
            c.start()
            copies[name, t, m] = c

    def received(t, m):
        copies["x", t, m].wait_recv()
        copies["y", t, m].wait_recv()

    def diagonal_out(t):
        ready(t * 4 + DG)

        def body(at):
            keep(to_x, t, 0, at, project(t * 4 + DG, 0, at), DG, 0)
            keep(to_y, t, 0, at, project(t * 4 + DG, 1, at), DG, 1)

        tiles(body)
        send_plane(t, 0)

    def raw_out(t):
        ready(t * 4 + XN)
        ready(t * 4 + YN)

        def body(at):
            keep(to_x, t, 1, at, project(t * 4 + XN, 0, at), XN, 0)
            keep(to_y, t, 1, at, project(t * 4 + YN, 1, at), YN, 1)

        tiles(body)
        send_plane(t, 1)

    def relay_out(t):
        received(t, 0)

        def body(at):
            keep(to_x, t, 2, at, project(t * 4 + XN, 1, at) + from_y[t, 0, span(t), at].astype(F32), XN, 1)
            keep(to_y, t, 2, at, project(t * 4 + YN, 0, at) + from_x[t, 0, span(t), at].astype(F32), YN, 0)

        tiles(body)
        send_plane(t, 2)

    def plane_sum(t, part, at):
        mx, my = (1, 2) if part == 0 else (2, 1)
        return (
            project(t * 4 + ME, part, at)
            + from_x[t, mx, span(t), at].astype(F32)
            + from_y[t, my, span(t), at].astype(F32)
        )

    def plane_ready(t):
        ready(t * 4 + ME)
        received(t, 1)
        received(t, 2)

    def z_copy(t, slot, dev):
        return remote(to_z.at[t], from_z.at[slot], szs_sem.at[t], szr_sem.at[slot], dev)

    def z_arrived(slot):
        z_copy(0, slot, pair).wait_recv()

    def z_fill(t, slots):
        def body(at):
            for part in (0, 1):
                v = plane_sum(t, part, at)
                for slot in slots:
                    v = v + from_z[slot, part, :, at].astype(F32)
                to_z[t, part, :, at] = v.astype(BF)

        tiles(body)

    def outer_send(t, slot):
        @pl.when(jnp.logical_not(inner))
        def _():
            z_fill(t, ())
            z_copy(t, slot, pair).start()

    def inner_send(t, add, slot, dev):
        @pl.when(inner)
        def _():
            z_arrived(add)
            z_fill(t, (add,))
            z_copy(t, slot, dev).start()

    def e_copy(t, slot, dev):
        return remote(to_e.at[t], from_e.at[slot], es_sem.at[t], er_sem.at[slot], dev)

    def e_arrived(slot):
        e_copy(0, slot, pair).wait_recv()

    def e_fill(t, slots):
        for q in range(4):

            def body(at, q=q):
                for part in (0, 1):
                    to = pl.ds(part * late, late)
                    v = project(t * 4 + q, part, at, pl.ds(part * hid + early, late))
                    for slot in slots:
                        v = v + from_e[slot, q, to, at].astype(F32)
                    to_e[t, q, to, at] = v.astype(BF)

            tiles(body)

    def e_outer(t, slot):
        @pl.when(jnp.logical_not(inner))
        def _():
            e_fill(t, ())
            e_copy(t, slot, pair).start()

    def e_inner(t, add, slot, dev):
        @pl.when(inner)
        def _():
            e_arrived(add)
            e_fill(t, (add,))
            e_copy(t, slot, dev).start()

    def e_total():
        e_arrived(4)

        @pl.when(jnp.logical_not(inner))
        def _():
            ends_sum[...] = from_e[4].astype(F32)

        @pl.when(inner)
        def _():
            e_arrived(3)
            ends_sum[...] = from_e[4].astype(F32) + from_e[3].astype(F32)


    listed[...] = jnp.where(mask[...] > 0, ids[...], -1)
    fan = ids.shape[0]
    tall = 128
    next_block = [0]

    def count(blocks):
        first = next_block[0]
        next_block[0] = first + blocks

        def body(i, carry):
            b = i // (rows // tall)
            r = pl.multiple_of(lax.rem(i, rows // tall) * tall, tall)
            base = b * rows + r
            node = lax.broadcasted_iota(jnp.int32, (tall, rows), 0).astype(BF)
            one, zero = jnp.ones((tall, rows), BF), jnp.zeros((tall, rows), BF)
            acc = zero
            for k in range(fan):
                rel = listed[pl.ds(k, 1), :] - base
                rel = jnp.where((rel >= 0) & (rel < tall), rel, -1).astype(F32)
                rel = jnp.broadcast_to(rel, (tall, rows)).astype(BF)
                acc = acc + jnp.where(rel == node, one, zero)
            edges[b, pl.ds(r, tall), :] = acc
            return carry

        lax.fori_loop(first * (rows // tall), (first + blocks) * (rows // tall), body, 0)

    fetch(0)
    w_copy.wait_recv()
    diagonal_out(0)
    raw_out(0)
    fetch(1)
    diagonal_out(1)
    fetch(2)
    fetch(3)
    for slot in (3, 7):
        ready(slot)
    e_outer(0, 0)
    count(3)
    relay_out(0)
    raw_out(1)
    diagonal_out(2)
    e_outer(1, 1)
    for slot in (9, 10, 11):
        ready(slot)
    e_outer(2, 4)
    e_inner(0, 0, 2, facing)
    count(3)
    relay_out(1)
    raw_out(2)
    e_inner(2, 2, 4, pair)
    e_inner(1, 1, 3, facing)
    count(3)
    plane_ready(0)
    outer_send(0, 0)
    count(7)
    e_total()
    relay_out(2)
    diagonal_out(3)
    raw_out(3)
    count(3)
    inner_send(0, 0, 2, facing)
    count(3)
    plane_ready(1)
    outer_send(1, 1)
    count(5)
    plane_ready(2)
    outer_send(2, 4)
    inner_send(2, 2, 4, pair)
    inner_send(1, 1, 3, facing)
    count(2)
    relay_out(3)
    count(3)
    assert next_block[0] == edges.shape[0]
    plane_ready(3)
    z_arrived(4)

    mine = (z, core, spot)

    def last(part, slots, out_ref):
        def body(at):
            v = plane_sum(3, part, at)
            w = v[:early]
            for slot in slots:
                w = w + from_z[slot, part, :, at].astype(F32)
            out_ref[main, at] = w.astype(out_ref.dtype)
            out_ref[ends, at] = (v[early:] + ends_sum[ME, pl.ds(part * late, late), at]).astype(out_ref.dtype)

        tiles(body)

    @pl.when(jnp.logical_not(inner))
    def _():
        last(0, (4,), full.at[0, z, core, spot])

    @pl.when(inner)
    def _():
        z_arrived(3)
        last(0, (4, 3), full.at[0, z, core, spot])

    def finish_scatter():
        @pl.when(jnp.logical_not(inner))
        def _():
            last(1, (4,), self1)

        @pl.when(inner)
        def _():
            last(1, (4, 3), self1)

        w_copy.wait_send()
        for c in mate_copies.values():
            c.wait_send()
        for c in copies.values():
            c.wait_send()
        for t in range(3):
            z_copy(t, 0, pair).wait_send()
            e_copy(t, 0, pair).wait_send()


    top, bottom = pl.ds(0, early // 2), pl.ds(early // 2, early // 2)
    ends_top, ends_bottom = pl.ds(early, late // 2), pl.ds(early + late // 2, late // 2)
    spot_x, spot_y = y * 2 + 1 - x, (1 - y) * 2 + x
    spot_d = 3 - spot

    def average(p, after_start):
        started = []

        def go(ref, send_sem, recv_sem, dev):
            c = remote(ref, ref, send_sem, recv_sem, dev)
            c.start()
            started.append(c)

        def piece(k, q, part, c=core):
            return full.at[p, planes[k], c, q, part]

        def arrived(dst, recv_sem):
            remote(dst, dst, xs_sem.at[p, 0], recv_sem, mate).wait_recv()

        def add(k, q, c=core, first=False):
            ref = full.at[p, planes[k], c, q]
            b = planes[k] * 8 + q * 2 + c

            def body(at):
                part = jnp.dot(ref[...], edges[b, :, at], preferred_element_type=F32)
                total[:, at] = part if first else total[:, at] + part

            tiles(body)

        hops = []

        def hop(ref, send, slot, dev):
            c = remote(ref, ref, zs_sem.at[p, send], zr_sem.at[p, slot], dev)

            @pl.when(inner)
            def _():
                c.start()

            hops.append(c)

        def to_plane(ref_x, ref_y, n):
            go(ref_x, xs_sem.at[p, n], xr_sem.at[p, n], xn)
            go(ref_y, ys_sem.at[p, n], yr_sem.at[p, n], yn)

        def to_mate(ref, n):
            go(ref, cs_sem.at[p, n], cr_sem.at[p, n], mate)

        def all_ends(k, c=core):
            return full.at[p, planes[k], c, :, ends]

        go(piece(0, spot, main), zs_sem.at[p, 0], zr_sem.at[p, 0], pair)
        hop(piece(0, spot, main), 1, 1, facing)
        to_plane(piece(0, spot, ends), piece(0, spot, ends), 8)
        to_plane(piece(0, spot, top), piece(0, spot, bottom), 0)
        to_mate(full.at[p, z, core, spot], 0)
        arrived(piece(0, spot_x, ends), xr_sem.at[p, 8])
        arrived(piece(0, spot_y, ends), yr_sem.at[p, 8])
        to_plane(piece(0, spot_y, ends_bottom), piece(0, spot_x, ends_top), 9)
        to_plane(piece(0, spot, bottom), piece(0, spot, top), 10)
        to_mate(piece(0, spot_x, ends), 20)
        to_mate(piece(0, spot_y, ends), 21)
        after_start()
        add(0, spot, first=True)

        def column(k):
            ref = piece(k, spot, main)
            arrived(ref, zr_sem.at[p, k - 1])
            if k == 1:
                hop(ref, 2, 2, facing)
            else:
                hop(ref, k + 1, k - 1, pair)
            to_plane(ref, ref, k)
            to_mate(ref, k)

        def own_ends():
            arrived(piece(0, spot_d, ends_top), yr_sem.at[p, 9])
            arrived(piece(0, spot_d, ends_bottom), xr_sem.at[p, 9])
            go(all_ends(0), zs_sem.at[p, 5], zr_sem.at[p, 3], pair)
            hop(all_ends(0), 6, 4, facing)
            to_mate(piece(0, spot_d, ends), 22)

        def ends_of(k):
            ref = all_ends(k)
            arrived(ref, zr_sem.at[p, 2 + k])
            if k == 1:
                hop(ref, 7, 5, facing)
            else:
                hop(ref, 6 + k, 2 + k, pair)
            to_mate(ref, 23 + k)
            add(k, spot)

        def relay(k):
            if k == 0:
                arrived(piece(0, spot_x, top), xr_sem.at[p, 0])
                arrived(piece(0, spot_y, bottom), yr_sem.at[p, 0])
                to_plane(piece(0, spot_y, bottom), piece(0, spot_x, top), 4)
                arrived(piece(0, spot_x, bottom), xr_sem.at[p, 10])
                arrived(piece(0, spot_y, top), yr_sem.at[p, 10])
            else:
                arrived(piece(k, spot_x, main), xr_sem.at[p, k])
                arrived(piece(k, spot_y, main), yr_sem.at[p, k])
                to_plane(piece(k, spot_y, bottom), piece(k, spot_x, top), 4 + k)
            to_mate(piece(k, spot_x, main), 4 + k)
            to_mate(piece(k, spot_y, main), 8 + k)
            add(k, spot_x)
            add(k, spot_y)

        def diagonal(k):
            arrived(piece(k, spot_d, top), yr_sem.at[p, 4 + k])
            to_mate(piece(k, spot_d, top), 12 + k)
            arrived(piece(k, spot_d, bottom), xr_sem.at[p, 4 + k])
            to_mate(piece(k, spot_d, bottom), 16 + k)
            add(k, spot_d)

        other = 1 - core

        def from_mate(k):
            if k == 0:
                arrived(full.at[p, z, other, spot], cr_sem.at[p, 0])
                arrived(piece(0, spot_x, ends, other), cr_sem.at[p, 20])
                arrived(piece(0, spot_y, ends, other), cr_sem.at[p, 21])
            else:
                arrived(all_ends(k, other), cr_sem.at[p, 23 + k])
                arrived(piece(k, spot, main, other), cr_sem.at[p, k])
            add(k, spot, other)
            arrived(piece(k, spot_x, main, other), cr_sem.at[p, 4 + k])
            add(k, spot_x, other)
            arrived(piece(k, spot_y, main, other), cr_sem.at[p, 8 + k])
            add(k, spot_y, other)

        def from_mate_diagonal(k):
            if k == 0:
                arrived(piece(0, spot_d, ends, other), cr_sem.at[p, 22])
            arrived(piece(k, spot_d, top, other), cr_sem.at[p, 12 + k])
            arrived(piece(k, spot_d, bottom, other), cr_sem.at[p, 16 + k])
            add(k, spot_d, other)

        own_ends()
        column(1)
        relay(0)
        column(2)
        ends_of(1)
        relay(1)
        column(3)
        from_mate(0)
        diagonal(0)
        ends_of(2)
        relay(2)
        from_mate(1)
        diagonal(1)
        from_mate_diagonal(0)
        ends_of(3)
        relay(3)
        from_mate(2)
        from_mate_diagonal(1)
        diagonal(2)
        from_mate(3)
        from_mate_diagonal(2)
        diagonal(3)
        from_mate_diagonal(3)

        def finish():
            for c in started:
                c.wait_send()

            @pl.when(inner)
            def _():
                for c in hops:
                    c.wait_send()

        return finish

    def mean():
        return total[...] * (1.0 / jnp.sum(mask[...].astype(F32), axis=0, keepdims=True))

    def across_rows(w, v):
        return lax.dot_general(w[...], v, (((0,), (0,)), ((), ())), preferred_element_type=F32)

    def put(p, v):
        full[(p,) + mine] = jnp.maximum(v, 0.0).astype(BF)

    def self_two():
        self1[...] = across_rows(w_self2, full[(1,) + mine])

    def self_three():
        out[...] = jnp.dot(w_self3[...], full[(0,) + mine], preferred_element_type=F32)

    finish = average(0, finish_scatter)
    put(1, self1[...] + mean())
    finish()
    finish = average(1, self_two)
    put(0, self1[...] + across_rows(w_nbr2, mean().astype(BF)))
    finish()
    finish = average(0, self_three)
    out[...] += jnp.dot(w_nbr3[...], mean().astype(BF), preferred_element_type=F32)
    finish()


def solution(mesh):
    def device_step(feat, w_self1, w_nbr1, ids, mask, w_self2, w_nbr2, w_self3, w_nbr3):
        rows, fan = ids.shape
        nodes, depth = feat.shape
        n = nodes // rows
        hid, classes = w_self3.shape
        vmem = pl.BlockSpec(memory_space=pltpu.VMEM)
        dma = pltpu.SemaphoreType.DMA
        logits = pl.pallas_call(
            kernel,
            out_shape=jax.ShapeDtypeStruct((classes, rows), F32),
            in_specs=[pl.BlockSpec(memory_space=pl.ANY)] + [vmem] * 7,
            out_specs=vmem,
            scratch_shapes=[
                pltpu.VMEM((16, depth, rows), BF),
                pltpu.VMEM((16, depth, rows), BF),
                pltpu.VMEM((2 * hid, depth), BF),
                pltpu.VMEM((4, 3, hid, rows), BF),
                pltpu.VMEM((4, 3, hid, rows), BF),
                pltpu.VMEM((4, 3, hid, rows), BF),
                pltpu.VMEM((4, 3, hid, rows), BF),
                pltpu.VMEM((3, 2, hid - 32, rows), BF),
                pltpu.VMEM((5, 2, hid - 32, rows), BF),
                pltpu.VMEM((3, 4, 64, rows), BF),
                pltpu.VMEM((5, 4, 64, rows), BF),
                pltpu.VMEM((4, 64, rows), F32),
                pltpu.VMEM((fan, rows), jnp.int32),
                pltpu.VMEM((n, rows, rows), BF),
                pltpu.VMEM((2, 4, 2, 4, hid, rows), BF),
                pltpu.VMEM((hid, rows), F32),
                pltpu.VMEM((hid, rows), F32),
                dma((16,)), dma((16,)), dma((16,)), dma((2,)),
                dma((4, 3)), dma((4, 3)), dma((4, 3)), dma((4, 3)), dma((3,)), dma((5,)), dma((3,)), dma((5,)),
                dma((2, 11)), dma((2, 11)), dma((2, 11)), dma((2, 11)), dma((2, 10)), dma((2, 6)), dma((2, 27)), dma((2, 27)),
            ],
            compiler_params=pltpu.CompilerParams(collective_id=0, has_side_effects=True, vmem_limit_bytes=67043328),
            name="sage",
        )(feat.T, jnp.concatenate([w_nbr1.T, w_self1.T], axis=0), ids.T, mask.T, w_self2, w_nbr2, w_self3.T, w_nbr3.T)
        return logits.T

    col_split, row_split, replicated = P(None, "g"), P("g", None), P()
    return jax.shard_map(
        device_step,
        mesh=mesh,
        in_specs=(col_split, row_split, row_split, row_split, row_split, replicated, replicated, replicated, replicated),
        out_specs=row_split,
        check_vma=False,
    )
```

time: 207 us -> 193 us (0.932)
  Pallas kernels: 203 us -> 188 us
    pallas_call x1, Pallas kernels: 203 us -> 188 us  [device_step(): pl.pallas_call(kernel, out_shape=jax.ShapeDtypeStruct((classes, rows), F3...]
where the time goes in v3:
time: 193 us
  Pallas kernels  188 us (97%)
  local copies, waits for them, and re-layouts  3.47 us (2%)
    pallas_call x1, Pallas kernels, device_step(): pl.pallas_call(kernel, out_shape=jax.ShapeDtypeStruct((classes, rows), F3...  188 us

profile of v3, /device:TPU:1, one launch (start us, length us, event | category | flops | bytes accessed | tf_op | source)
XLA Modules:
  0.0 192.7 jit_solution(15939037957721532561)
XLA Ops:
  0.0 1.1 copy.11
  1.1 1.1 copy.10
  2.2 0.8 pad_maximum_fusion.w_ref
  2.9 188.4 %sage.1 = f32[5,512]{1,0:T(8,128)} custom-call(bf16[264,16384]{1,0:T(8,128)(2,1)} %bitcast.8, bf16[512,264]{1,0:T(8,128)(2,1)} %pad_maximum_fusion.w_ref, s32[15,512]{1,0:T(8,128)} %bitcast.12, s32[15,512]{1,0:T(8,128)} %bitcast.13, bf16[256,256]{1,0:T(8,128)(2,1)} %w_self2.1, bf16[256,256]{1,0:T(8,128)(2,1)} %w_nbr2.1, bf16[5,256]{1,0:T(8,128)(2,1)} %bitcast.14, ...), custom_call_target="tpu_custom_call" | custom-call | tf_op jit(solution)/shard_map/sage/pallas_call | solution.py:561
  191.4 1.3 copy.13

commit v4 on v3

--- a/solution.py
+++ b/solution.py
@@ -18,8 +18,8 @@
 
 
 def kernel(
-    feat, w_ref, ids, mask, w_self2, w_nbr2, w_self3, w_nbr3, out,
-    own, got, w_got, to_x, to_y, from_x, from_y, to_z, from_z, to_e, from_e, ends_sum, listed, edges, full, total, self1,
+    feat, w_nbr1, w_self1, ids, mask, w_self2, w_nbr2, w_self3, w_nbr3, out,
+    own, got, w_ref, w_got, to_x, to_y, from_x, from_y, to_z, from_z, to_e, from_e, ends_sum, listed, edges, full, total, self1,
     own_sem, gs_sem, gr_sem, w_sem, sxs_sem, sxr_sem, sys_sem, syr_sem, szs_sem, szr_sem, es_sem, er_sem,
     xs_sem, xr_sem, ys_sem, yr_sem, zs_sem, zr_sem, cs_sem, cr_sem,
 ):
@@ -60,6 +60,8 @@
         lax.fori_loop(0, rows // chunk, step, 0)
 
 
+    for part, w in ((0, w_nbr1), (1, w_self1)):
+        w_ref[pl.ds(part * hid, hid), :] = jnp.transpose(w[...].astype(F32)).astype(BF)
     w_copy = remote(w_ref, w_got, w_sem.at[0], w_sem.at[1], mate)
     w_copy.start()
     own_copies, mate_copies = {}, {}
@@ -371,13 +373,14 @@
         def arrived(dst, recv_sem):
             remote(dst, dst, xs_sem.at[p, 0], recv_sem, mate).wait_recv()
 
-        def add(k, q, c=core, first=False):
-            ref = full.at[p, planes[k], c, q]
-            b = planes[k] * 8 + q * 2 + c
-
+        def add(k, *places, c=core, first=False):
             def body(at):
-                part = jnp.dot(ref[...], edges[b, :, at], preferred_element_type=F32)
-                total[:, at] = part if first else total[:, at] + part
+                part = None if first else total[:, at]
+                for q in places:
+                    b = planes[k] * 8 + q * 2 + c
+                    term = jnp.dot(full[p, planes[k], c, q], edges[b, :, at], preferred_element_type=F32)
+                    part = term if part is None else part + term
+                total[:, at] = part
 
             tiles(body)
 
@@ -441,7 +444,6 @@
             else:
                 hop(ref, 6 + k, 2 + k, pair)
             to_mate(ref, 23 + k)
-            add(k, spot)
 
         def relay(k):
             if k == 0:
@@ -456,8 +458,6 @@
                 to_plane(piece(k, spot_y, bottom), piece(k, spot_x, top), 4 + k)
             to_mate(piece(k, spot_x, main), 4 + k)
             to_mate(piece(k, spot_y, main), 8 + k)
-            add(k, spot_x)
-            add(k, spot_y)
 
         def diagonal(k):
             arrived(piece(k, spot_d, top), yr_sem.at[p, 4 + k])
@@ -476,36 +476,38 @@
             else:
                 arrived(all_ends(k, other), cr_sem.at[p, 23 + k])
                 arrived(piece(k, spot, main, other), cr_sem.at[p, k])
-            add(k, spot, other)
             arrived(piece(k, spot_x, main, other), cr_sem.at[p, 4 + k])
-            add(k, spot_x, other)
             arrived(piece(k, spot_y, main, other), cr_sem.at[p, 8 + k])
-            add(k, spot_y, other)
+            add(k, spot, spot_x, spot_y, c=other)
 
         def from_mate_diagonal(k):
             if k == 0:
                 arrived(piece(0, spot_d, ends, other), cr_sem.at[p, 22])
             arrived(piece(k, spot_d, top, other), cr_sem.at[p, 12 + k])
             arrived(piece(k, spot_d, bottom, other), cr_sem.at[p, 16 + k])
-            add(k, spot_d, other)
+            add(k, spot_d, c=other)
 
         own_ends()
         column(1)
         relay(0)
+        add(0, spot_x, spot_y)
         column(2)
         ends_of(1)
         relay(1)
+        add(1, spot, spot_x, spot_y)
         column(3)
+        ends_of(2)
         from_mate(0)
         diagonal(0)
-        ends_of(2)
         relay(2)
+        add(2, spot, spot_x, spot_y)
+        ends_of(3)
         from_mate(1)
         diagonal(1)
         from_mate_diagonal(0)
-        ends_of(3)
+        from_mate(2)
         relay(3)
-        from_mate(2)
+        add(3, spot, spot_x, spot_y)
         from_mate_diagonal(1)
         diagonal(2)
         from_mate(3)
@@ -561,11 +563,12 @@
         logits = pl.pallas_call(
             kernel,
             out_shape=jax.ShapeDtypeStruct((classes, rows), F32),
-            in_specs=[pl.BlockSpec(memory_space=pl.ANY)] + [vmem] * 7,
+            in_specs=[pl.BlockSpec(memory_space=pl.ANY)] + [vmem] * 8,
             out_specs=vmem,
             scratch_shapes=[
                 pltpu.VMEM((16, depth, rows), BF),
                 pltpu.VMEM((16, depth, rows), BF),
+                pltpu.VMEM((2 * hid, depth), BF),
                 pltpu.VMEM((2 * hid, depth), BF),
                 pltpu.VMEM((4, 3, hid, rows), BF),
                 pltpu.VMEM((4, 3, hid, rows), BF),
@@ -587,7 +590,7 @@
             ],
             compiler_params=pltpu.CompilerParams(collective_id=0, has_side_effects=True, vmem_limit_bytes=67043328),
             name="sage",
-        )(feat.T, jnp.concatenate([w_nbr1.T, w_self1.T], axis=0), ids.T, mask.T, w_self2, w_nbr2, w_self3.T, w_nbr3.T)
+        )(feat.T, w_nbr1, w_self1, ids.T, mask.T, w_self2, w_nbr2, w_self3.T, w_nbr3.T)
         return logits.T
 
     col_split, row_split, replicated = P(None, "g"), P("g", None), P()

time: 193 us -> 186 us (0.964)
  Pallas kernels: 188 us -> 185 us
  local copies, waits for them, and re-layouts: 3.47 us -> 1.32 us
    pallas_call x1, Pallas kernels: 188 us -> 185 us  [device_step(): pl.pallas_call(kernel, out_shape=jax.ShapeDtypeStruct((classes, rows), F3...]
    unnamed x3 -> x1, local copies, waits for them, and re-layouts: 3.47 us -> 1.32 us
where the time goes in v4:
time: 186 us
  Pallas kernels  185 us (99%)
    pallas_call x1, Pallas kernels, device_step(): pl.pallas_call(kernel, out_shape=jax.ShapeDtypeStruct((classes, rows), F3...  185 us

profile of v4, /device:TPU:1, one launch (start us, length us, event | category | flops | bytes accessed | tf_op | source)
XLA Modules:
  0.0 185.9 jit_solution(2219921400583764709)
XLA Ops:
  0.0 184.5 %sage.1 = f32[5,512]{1,0:T(8,128)} custom-call(bf16[264,16384]{1,0:T(8,128)(2,1)} %bitcast.6, bf16[264,256]{1,0:T(8,128)(2,1)} %w_nbr1.1, bf16[264,256]{1,0:T(8,128)(2,1)} %w_self1.1, s32[15,512]{1,0:T(8,128)} %bitcast.8, s32[15,512]{1,0:T(8,128)} %bitcast.9, bf16[256,256]{1,0:T(8,128)(2,1)} %w_self2.1, bf16[256,256]{1,0:T(8,128)(2,1)} %w_nbr2.1, ...), custom_call_target="tpu_custom_call" | custom-call | tf_op jit(solution)/shard_map/sage/pallas_call | solution.py:563
  184.5 1.3 copy.11
